TPU v7x, 256 devices: a whole 4x4x8 slice. The times are simulated.
256 devices in a mesh: row: 32 (over z, x), col: 8 (over y, core).
Axes of the slice: x: 4, y: 4, z: 8, core: 2. Of those that a mesh axis runs over, the one named last changes fastest.
Arguments:
- integrals: bfloat16 [65536, 8192], P('row', 'col'), may hold values from -0.0234375 to 0.0234375
- lambda2: bfloat16 [2016, 65536], P('col', 'row'), may hold values from -6 to 6
- source_terms: float32 [2016, 8192], P('row', 'col'), may hold values from -6 to 6
- hist_amp: bfloat16 [5, 2016, 8192], P(None, 'row', 'col'), may hold values from -6 to 6
- hist_err: bfloat16 [5, 2016, 8192], P(None, 'row', 'col'), may hold values from -64 to 64
- eps_occ: float32 [64], replicated, may hold values from -1 to -0.3
- eps_vir: float32 [800], replicated, may hold values from 0.1 to 1
- occ_pair: int32 [2, 2016], P(None, 'row'), may hold values from 0 to 63, as said below
- vir_pair: int32 [2, 8192], P(None, 'col'), may hold values from 0 to 799, as said below
Outputs:
- updated: float32 [2016, 8192], P('row', 'col')
Inputs may be any that keep to these rules, and one draw needn't show every extreme that they name: `occ_pair`: every pair i < j of the 64 occupied orbitals appears exactly once, in some order. `vir_pair`: in every column the first orbital is smaller than the second.
All inputs are finite; a program needn't handle non-finite values.
Results may differ from a plain program's by a relative error of at most 0.0003.
Values may be sent and summed in bfloat16 or wider, within the bound.
A program may use at most 64 MiB of HBM per device.

v0:
```python
import jax
import jax.numpy as jnp
from jax import lax
from jax.sharding import PartitionSpec as P

precise = lax.Precision.HIGHEST


def pair_energy(pairs, energies):
    levels = jnp.arange(energies.shape[0], dtype=jnp.int32)
    first = jnp.sum(jnp.where(pairs[0][:, None] == levels[None, :], energies[None, :], 0.0), axis=1)
    second = jnp.sum(
        jnp.where(pairs[1][:, None] == levels[None, :], energies[None, :], 0.0), axis=1
    )
    return first + second


def diis_weights(correlation):
    factor = jnp.linalg.cholesky(correlation)
    order = correlation.shape[0]
    forward = []
    for k in range(order):
        running = jnp.ones((), correlation.dtype)
        for m in range(k):
            running = running - factor[k, m] * forward[m]
        forward.append(running / factor[k, k])
    backward = [None] * order
    for k in reversed(range(order)):
        running = forward[k]
        for m in range(k + 1, order):
            running = running - factor[m, k] * backward[m]
        backward[k] = running / factor[k, k]
    solved = jnp.stack(backward)
    return solved / jnp.sum(solved)


def on_device(
    integrals, lambda2, source_terms, hist_amp, hist_err, eps_occ, eps_vir, occ_pair, vir_pair
):
    stored_count = hist_err.shape[0]
    flat_stored = hist_err.astype(jnp.float32).reshape(stored_count, -1)
    all_cols = lax.all_gather(lambda2, "col", axis=0, tiled=True)
    ladder = lax.psum_scatter(
        jnp.dot(all_cols, integrals, preferred_element_type=jnp.float32),
        "row",
        scatter_dimension=0,
        tiled=True,
    )
    denominator = pair_energy(occ_pair, eps_occ)[:, None] - pair_energy(vir_pair, eps_vir)[None, :]
    raw_update = (source_terms + ladder) / denominator
    err_new = raw_update - hist_amp[0].astype(jnp.float32)
    flat_new = err_new.reshape(1, -1)
    stacked = jnp.concatenate([flat_stored, flat_new], axis=0)
    correlation = lax.psum(jnp.dot(stacked, stacked.T, precision=precise), ("row", "col"))
    weights = diis_weights(correlation)
    updated = weights[stored_count] * raw_update
    for k in range(stored_count):
        updated = updated + weights[k] * hist_amp[k].astype(jnp.float32)
    return updated


def solution(mesh):
    placed = (
        P("row", "col"),
        P("col", "row"),
        P("row", "col"),
        P(None, "row", "col"),
        P(None, "row", "col"),
        P(),
        P(),
        P(None, "row"),
        P(None, "col"),
    )
    return jax.shard_map(
        on_device, mesh=mesh, in_specs=placed, out_specs=P("row", "col"), check_vma=False
    )
```

profile of v0, /device:TPU:1, one launch (start us, length us, event | category | flops | bytes accessed | tf_op | source)
XLA Modules:
  0.0 320.9 jit_solution(15406420744793112163)
XLA Ops:
  6.5 0.0 all-gather.3.cloned.1.call-start
  6.5 0.7 all-gather.3.cloned.1.call-update
  7.3 0.8 fusion.14
  8.0 1.5 select_reduce_fusion
  9.6 1.2 convert_bitcast_fusion
  10.8 54.8 %all-gather.3.cloned.1.call-done = bf16[8,252,2048]{2,1,0:T(8,128)(2,1)} async-done(((bf16[1,252,2048]{2,1,0:T(8,128)(2,1)}), bf16[8,252,2048]{2,1,0:T(8,128)(2,1)}) %all-gather.3.cloned.1.call-update) | async-done | bytes 8257552 | tf_op jit(solution)/shard_map/all_gather | solution.py:42
  65.7 7.5 %reshape.68 = bf16[2016,2048]{1,0:T(8,128)(2,1)} reshape(bf16[8,252,2048]{2,1,0:T(8,128)(2,1)} %all-gather.3.cloned.1.call-done) | data formatting | bytes 16515072
  73.1 14.2 %fusion.18 = f32[2016,1024]{1,0:T(8,128)} fusion(bf16[2016,2048]{1,0:T(8,128)(2,1)} %reshape.68, bf16[2048,1024]{1,0:T(8,128)(2,1)} %param.9), kind=kOutput, calls=%fused_computation.38 | convolution fusion | flops 8455716864 | bytes 20709376 | tf_op jit(solution)/shard_map/dot_general | solution.py:44
  87.4 0.0 copy-start.3
  87.4 100.2 %fusion = f32[64,1024]{1,0:T(8,128)S(1)} fusion(f32[2016,1024]{1,0:T(8,128)} %fusion.18), kind=kCustom, calls=%all-reduce-scatter | all-reduce-scatter fusion | flops 2097153 | bytes 8520704
  187.6 0.0 copy-start
  187.6 0.0 copy-start.5
  187.6 0.0 copy-start.4
  187.6 2.3 collective-permute-start
  189.9 0.0 copy-done.3
  190.0 0.0 copy-done
  190.0 0.8 copy.19
  190.8 0.0 copy-done.5
  190.8 0.0 copy-start.1
  190.8 0.0 copy-start.2
  190.8 0.6 dynamic-slice.4
  191.9 0.0 copy-done.4
  192.0 0.2 select_reduce_fusion.2
  192.2 0.0 collective-permute-done
  192.2 2.0 concatenate.4
  194.2 1.1 fusion.5
  195.3 0.3 copy.20
  195.6 4.5 %fusion.1 = f32[6,6]{0,1:T(8,128)S(1)} fusion(f32[1,64512]{1,0:T(1,128)S(1)} %bitcast.70, f32[5,64512]{1,0:T(8,128)S(1)} %bitcast.68), kind=kOutput, calls=%fused_computation.4 | convolution fusion | flops 28256256 | bytes 1548432 | tf_op jit(solution)/shard_map/dot_general | solution.py:54
  200.1 78.7 %psum.7 = f32[6,6]{0,1:T(8,128)S(1)} all-reduce(f32[6,6]{0,1:T(8,128)S(1)} %fusion.1), channel_id=1, replica_groups=mesh['row'=32,'col'=8] {'row','col'}, use_global_device_ids=true, to_apply=%region_5.6 | all-reduce | flops 36 | bytes 288 | tf_op jit(solution)/shard_map/psum | solution.py:54
  278.8 0.1 copy.17
  278.9 0.5 cholesky.18
  279.4 0.6 compare_reduce_fusion
  280.1 0.6 select_select_fusion
  280.7 0.6 fusion.16
  281.3 0.7 fusion.15
  308.7 0.1 stack.27
  308.7 0.7 fusion.17
  309.4 0.0 copy-done.1
  309.4 0.0 copy-done.2
  309.4 4.6 %fusion.10 = f32[63,1024]{1,0:T(8,128)} fusion(bf16[5,63,1024]{2,1,0:T(8,128)(2,1)S(1)} %copy-done.2, f32[]{:T(128)} %bitcast.43, f32[]{:T(128)} %bitcast.41, f32[]{:T(128)} %bitcast.39, f32[]{:T(128)} %bitcast.37, f32[]{:T(128)} %bitcast.35, f32[]{:T(128)} %bitcast.34, f32[1024]{0:T(1024)S(1)} %add.47, f32[63]{0:T(128)S(1)} %add.46, ...), kind=kLoop, calls=%fused_computation.16 | loop fusion | flops 1225728 | bytes 1423640 | tf_op jit(solution)/shard_map/add | solution.py:58
  (7 shorter events, 0.1 us)
Async XLA Ops:
  6.5 59.1 %all-gather.3.cloned.1.call-start = ((), (), s32[]{:S(2)}) async-start(), calls=%async_computation | async-start | bytes 9437184 | tf_op jit(solution)/shard_map/all_gather | solution.py:42
  87.4 102.6 %copy-start.3 = (s32[2,63]{1,0:T(2,128)S(1)}, s32[2,63]{1,0:T(2,128)}, u32[]{:S(2)}) copy-start(s32[2,63]{1,0:T(2,128)} %param.16) | copy-start | bytes 1516
  187.6 2.4 copy-start
  187.6 3.2 copy-start.5
  187.6 4.3 %copy-start.4 = (f32[64]{0:T(128)S(1)}, f32[64]{0:T(128)}, u32[]{:S(2)}) copy-start(f32[64]{0:T(128)} %param.14) | copy-start | bytes 772
  187.6 4.5 %collective-permute-start = (f32[31,1024]{1,0:T(8,128)S(1)}, f32[31,1024]{1,0:T(8,128)}, u32[]{:S(2)}, u32[]{:S(2)}) collective-permute-start(f32[31,1024]{1,0:T(8,128)S(1)} %slice.172), channel_id=1, source_target_pairs={{0,8},{8,16},{16,24},{24,32},{32,40},{40,48},{48,56},{56,64},{64,7... | collective-permute-start | bytes 380936
  190.8 118.6 %copy-start.1 = (f32[63,1024]{1,0:T(8,128)S(1)}, f32[63,1024]{1,0:T(8,128)}, u32[]{:S(2)}) copy-start(f32[63,1024]{1,0:T(8,128)} %param.11) | copy-start | bytes 774148
  190.8 118.6 %copy-start.2 = (bf16[5,63,1024]{2,1,0:T(8,128)(2,1)S(1)}, bf16[5,63,1024]{2,1,0:T(8,128)(2,1)}, u32[]{:S(2)}) copy-start(bf16[5,63,1024]{2,1,0:T(8,128)(2,1)} %param.12) | copy-start | bytes 1935364
Sparse Core Ops, SparseCore 0:
  9.2 56.4 all-gather.2
where the time goes:
time: 322 us; the launch traced here: 321 us
  blocking collectives  179 us (56%)
  waiting for transfers between devices  55.6 us (17%)
  between operations  40.7 us (13%)
  matrix products  18.7 us (6%)
  local copies, waits for them, and re-layouts  14.1 us (4%)
  other arithmetic  10.6 us (3%)
    unnamed x1, blocking collectives  100 us
    psum x1, blocking collectives, on_device(): lax.psum(jnp.dot(stacked, stacked.T, precision=precise), ('row', 'col'))  78.7 us
    all_gather x1, waiting for transfers between devices, on_device(): all_cols = lax.all_gather(lambda2, 'col', axis=0, tiled=True)  54.8 us
    dot_general x1, matrix products, on_device(): jnp.dot(all_cols, integrals, preferred_element_type=jnp.float32)  14.2 us
    unnamed x18, local copies, waits for them, and re-layouts  11.2 us
  transfers between devices with their start and end apart: 2, of which 1 were waited for; matrix products, arithmetic and copies ran while one was open for 2% of the time, Pallas kernels for 0%

commit v1 on v0

--- a/solution.py
+++ b/solution.py
@@ -51,7 +51,7 @@
     err_new = raw_update - hist_amp[0].astype(jnp.float32)
     flat_new = err_new.reshape(1, -1)
     stacked = jnp.concatenate([flat_stored, flat_new], axis=0)
-    correlation = lax.psum(jnp.dot(stacked, stacked.T, precision=precise), ("row", "col"))
+    correlation = lax.psum(lax.psum(jnp.dot(stacked, stacked.T, precision=precise), "col"), "row")
     weights = diis_weights(correlation)
     updated = weights[stored_count] * raw_update
     for k in range(stored_count):

time: 322 us -> 330 us (1.025)
  the two profiles are of different devices: /device:TPU:1 before, /device:TPU:130 now
where the time goes in v1:
time: 330 us; the launch traced here: 329 us
  blocking collectives  186 us (56%)
  waiting for transfers between devices  56 us (17%)
  between operations  40.7 us (12%)
  matrix products  18.7 us (6%)
  local copies, waits for them, and re-layouts  14.1 us (4%)
  other arithmetic  10.6 us (3%)
    unnamed x1, blocking collectives  99.1 us
    psum x1, blocking collectives, on_device(): lax.psum(lax.psum(jnp.dot(stacked, stacked.T, precision=precise), 'col'),...  75 us
    all_gather x1, waiting for transfers between devices, on_device(): all_cols = lax.all_gather(lambda2, 'col', axis=0, tiled=True)  52.1 us
    dot_general x1, matrix products, on_device(): jnp.dot(all_cols, integrals, preferred_element_type=jnp.float32)  14.2 us
    psum x1, blocking collectives, on_device(): lax.psum(jnp.dot(stacked, stacked.T, precision=precise), 'col')  12.4 us
    unnamed x18, local copies, waits for them, and re-layouts  11.1 us
  transfers between devices with their start and end apart: 2, of which 2 were waited for; matrix products, arithmetic and copies ran while one was open for 2% of the time, Pallas kernels for 0%

profile of v1, /device:TPU:130, one launch (start us, length us, event | category | flops | bytes accessed | tf_op | source)
XLA Modules:
  0.0 328.7 jit_solution(9233556880754398183)
XLA Ops:
  6.5 0.0 all-gather.3.cloned.1.call-start
  6.5 0.7 all-gather.3.cloned.1.call-update
  7.3 0.8 fusion.14
  8.0 1.5 select_reduce_fusion
  9.6 1.2 convert_bitcast_fusion
  10.8 52.1 %all-gather.3.cloned.1.call-done = bf16[8,252,2048]{2,1,0:T(8,128)(2,1)} async-done(((bf16[1,252,2048]{2,1,0:T(8,128)(2,1)}), bf16[8,252,2048]{2,1,0:T(8,128)(2,1)}) %all-gather.3.cloned.1.call-update) | async-done | bytes 8257552 | tf_op jit(solution)/shard_map/all_gather | solution.py:42
  62.9 7.5 %reshape.68 = bf16[2016,2048]{1,0:T(8,128)(2,1)} reshape(bf16[8,252,2048]{2,1,0:T(8,128)(2,1)} %all-gather.3.cloned.1.call-done) | data formatting | bytes 16515072
  70.4 14.2 %fusion.18 = f32[2016,1024]{1,0:T(8,128)} fusion(bf16[2016,2048]{1,0:T(8,128)(2,1)} %reshape.68, bf16[2048,1024]{1,0:T(8,128)(2,1)} %param.9), kind=kOutput, calls=%fused_computation.38 | convolution fusion | flops 8455716864 | bytes 20709376 | tf_op jit(solution)/shard_map/dot_general | solution.py:44
  84.6 0.0 copy-start.3
  84.6 99.1 %fusion = f32[64,1024]{1,0:T(8,128)S(1)} fusion(f32[2016,1024]{1,0:T(8,128)} %fusion.18), kind=kCustom, calls=%all-reduce-scatter | all-reduce-scatter fusion | flops 2097153 | bytes 8520704
  183.7 0.0 copy-start
  183.8 0.0 copy-start.5
  183.8 0.0 copy-start.4
  183.8 2.1 collective-permute-start
  185.9 0.0 copy-done.3
  185.9 0.0 copy-done
  185.9 0.8 copy.19
  186.7 0.0 copy-done.5
  186.7 0.0 copy-start.1
  186.7 0.0 copy-start.2
  186.7 0.6 dynamic-slice.4
  187.9 0.0 copy-done.4
  187.9 0.2 select_reduce_fusion.2
  188.1 3.1 collective-permute-done
  191.2 2.0 concatenate.4
  193.2 1.1 fusion.5
  194.4 0.3 copy.20
  194.7 4.5 %fusion.1 = f32[6,6]{0,1:T(8,128)S(1)} fusion(f32[1,64512]{1,0:T(1,128)S(1)} %bitcast.70, f32[5,64512]{1,0:T(8,128)S(1)} %bitcast.68), kind=kOutput, calls=%fused_computation.4 | convolution fusion | flops 28256256 | bytes 1548432 | tf_op jit(solution)/shard_map/dot_general | solution.py:54
  199.2 12.4 %psum.14 = f32[6,6]{0,1:T(8,128)S(1)} all-reduce(f32[6,6]{0,1:T(8,128)S(1)} %fusion.1), channel_id=1, replica_groups=mesh['row'=32,'col'=8] {'col'}, use_global_device_ids=true, to_apply=%region_5.6 | all-reduce | flops 36 | bytes 288 | tf_op jit(solution)/shard_map/psum | solution.py:54
  211.6 75.0 %psum.15 = f32[6,6]{0,1:T(8,128)S(1)} all-reduce(f32[6,6]{0,1:T(8,128)S(1)} %psum.14), channel_id=1, replica_groups=mesh['row'=32,'col'=8] {'row'}, use_global_device_ids=true, to_apply=%region_6.7 | all-reduce | flops 36 | bytes 288 | tf_op jit(solution)/shard_map/psum | solution.py:54
  286.5 0.1 copy.17
  286.6 0.5 cholesky.18
  287.2 0.6 compare_reduce_fusion
  287.8 0.6 select_select_fusion
  288.5 0.6 fusion.16
  289.1 0.7 fusion.15
  316.4 0.1 stack.27
  316.5 0.7 fusion.17
  317.2 0.0 copy-done.1
  317.2 0.0 copy-done.2
  317.2 4.6 %fusion.10 = f32[63,1024]{1,0:T(8,128)} fusion(bf16[5,63,1024]{2,1,0:T(8,128)(2,1)S(1)} %copy-done.2, f32[]{:T(128)} %bitcast.43, f32[]{:T(128)} %bitcast.41, f32[]{:T(128)} %bitcast.39, f32[]{:T(128)} %bitcast.37, f32[]{:T(128)} %bitcast.35, f32[]{:T(128)} %bitcast.34, f32[1024]{0:T(1024)S(1)} %add.49, f32[63]{0:T(128)S(1)} %add.48, ...), kind=kLoop, calls=%fused_computation.16 | loop fusion | flops 1225728 | bytes 1423640 | tf_op jit(solution)/shard_map/add | solution.py:58
  (7 shorter events, 0.1 us)
Async XLA Ops:
  6.5 56.4 %all-gather.3.cloned.1.call-start = ((), (), s32[]{:S(2)}) async-start(), calls=%async_computation | async-start | bytes 9437184 | tf_op jit(solution)/shard_map/all_gather | solution.py:42
  84.6 101.2 %copy-start.3 = (s32[2,63]{1,0:T(2,128)S(1)}, s32[2,63]{1,0:T(2,128)}, u32[]{:S(2)}) copy-start(s32[2,63]{1,0:T(2,128)} %param.16) | copy-start | bytes 1516
  183.7 2.1 copy-start
  183.8 3.0 copy-start.5
  183.8 4.1 %copy-start.4 = (f32[64]{0:T(128)S(1)}, f32[64]{0:T(128)}, u32[]{:S(2)}) copy-start(f32[64]{0:T(128)} %param.14) | copy-start | bytes 772
  183.8 7.4 %collective-permute-start = (f32[31,1024]{1,0:T(8,128)S(1)}, f32[31,1024]{1,0:T(8,128)}, u32[]{:S(2)}, u32[]{:S(2)}) collective-permute-start(f32[31,1024]{1,0:T(8,128)S(1)} %slice.172), channel_id=1, source_target_pairs={{0,8},{8,16},{16,24},{24,32},{32,40},{40,48},{48,56},{56,64},{64,7... | collective-permute-start | bytes 380936
  186.7 130.5 %copy-start.1 = (f32[63,1024]{1,0:T(8,128)S(1)}, f32[63,1024]{1,0:T(8,128)}, u32[]{:S(2)}) copy-start(f32[63,1024]{1,0:T(8,128)} %param.11) | copy-start | bytes 774148
  186.7 130.5 %copy-start.2 = (bf16[5,63,1024]{2,1,0:T(8,128)(2,1)S(1)}, bf16[5,63,1024]{2,1,0:T(8,128)(2,1)}, u32[]{:S(2)}) copy-start(bf16[5,63,1024]{2,1,0:T(8,128)(2,1)} %param.12) | copy-start | bytes 1935364
Sparse Core Ops, SparseCore 0:
  9.2 53.7 all-gather.2
